TPU v7x, 32 devices: a whole 2x2x4 slice. The times are simulated.
32 devices in a mesh: seq: 8 (over z, y), head: 4 (over x, core).
Axes of the slice: x: 2, y: 2, z: 4, core: 2. Of those that a mesh axis runs over, the one named last changes fastest.
Arguments:
- queries: bfloat16 [2048, 8192], P('seq', 'head'), may hold values from -40 to 40
- key_rows: bfloat16 [2048, 8192], P('seq', 'head'), may hold values from -20 to 20
- value_rows: bfloat16 [2048, 8192], P('seq', 'head'), may hold values from -8 to 8
Outputs:
- attended: bfloat16 [2048, 8192], P('seq', 'head')
All inputs are finite; a program needn't handle non-finite values.
Results may differ from a plain program's by a relative error of at most 0.0043.
Values may be sent and summed in bfloat16 or wider, within the bound.
A program may use at most 128 MiB of HBM per device.

v0:
```python
from functools import reduce
import math

import jax
import jax.numpy as jnp
from jax import lax
from jax.sharding import PartitionSpec as P

HEAD_DIM = 128
BLOCK = 128
POOL = 64
MID_REACH = 3
FAR_REACH = 9


def passed_along(block, axis, distance):
    devices = range(lax.axis_size(axis))
    route = [(i - distance, i) for i in devices if i - distance in devices]
    return lax.ppermute(block, axis, route)


def padded(cells, sides, width):
    for axis, dim in sides:
        count = lax.axis_size(axis)
        ends = count - 1
        head = lax.slice_in_dim(cells, 0, width, axis=dim)
        tail = lax.slice_in_dim(cells, cells.shape[dim] - width, cells.shape[dim], axis=dim)
        cells = jnp.concatenate(
            [
                lax.ppermute(tail, axis, [(i, (i + 1) % count) for i in range(ends)]),
                cells,
                lax.ppermute(head, axis, [((i + 1) % count, i) for i in range(ends)]),
            ],
            axis=dim,
        )
    return cells


def pool_pairs(source):
    paired = source.astype(jnp.float32).reshape(
        source.shape[0], source.shape[1] // 2, 2, source.shape[2]
    )
    return (0.5 * (paired[:, :, 0] + paired[:, :, 1])).astype(jnp.bfloat16)


def pool_groups(source, group_rows):
    grouped = source.astype(jnp.float32).reshape(
        source.shape[0], source.shape[1] // group_rows, group_rows, source.shape[2]
    )
    return jnp.mean(grouped, axis=2).astype(jnp.bfloat16)


def keep_rows(piece, toward, kept_rows):
    if toward < 0:
        return piece[:, piece.shape[1] - kept_rows :]
    return piece[:, :kept_rows]


def reach_middle(source, toward, highest, kept_rows):
    collected = {}
    for distance in range(1, highest + 1):
        sending = keep_rows(source, toward, kept_rows) if distance == highest else source
        collected[distance] = passed_along(sending, "seq", -toward * distance)
    return collected


def reach_far(source, anchor_at, toward, lowest, highest, kept_rows):
    collected = {}
    for distance in range(max(lowest, anchor_at + 1), highest + 1):
        sending = keep_rows(source, toward, kept_rows) if distance == highest else source
        collected[distance] = passed_along(sending, "seq", -toward * distance)
    return collected


def per_device(queries, key_rows, value_rows):
    rows_dev = queries.shape[0]
    blocks_dev = rows_dev // BLOCK
    total_rows = rows_dev * lax.axis_size("seq")
    total_blocks = total_rows // BLOCK
    me_index = lax.axis_index("seq")
    mid_top = (MID_REACH + blocks_dev - 1) // blocks_dev
    far_top = (FAR_REACH + blocks_dev - 1) // blocks_dev
    near_far = (MID_REACH + 1) // blocks_dev
    far_low = max(1, near_far)
    half_block = BLOCK // 2
    quarter_block = BLOCK // 4
    far_blocks = blocks_dev
    if far_top <= mid_top:
        far_blocks = blocks_dev
    stacked = jnp.stack((key_rows, value_rows))
    pair_two = pool_pairs(stacked)
    pair_four = pool_pairs(pair_two)
    pair_coarse = pool_groups(pair_four, POOL // 4)
    fine_window = padded(stacked, (("seq", 1),), BLOCK)
    lower_mid = reach_middle(pair_two, -1, mid_top, blocks_dev * half_block)
    upper_mid = reach_middle(pair_two, 1, mid_top, blocks_dev * half_block)
    lower_far = {
        distance: pool_pairs(lower_mid[distance])
        for distance in range(far_low, min(mid_top, far_top) + 1)
    }
    upper_far = {
        distance: pool_pairs(upper_mid[distance])
        for distance in range(far_low, min(mid_top, far_top) + 1)
    }
    lower_far.update(
        reach_far(pair_four, mid_top, -1, far_low, far_top, far_blocks * quarter_block)
    )
    upper_far.update(reach_far(pair_four, mid_top, 1, far_low, far_top, far_blocks * quarter_block))
    coarse_all = lax.all_gather(pair_coarse, "seq", axis=1, tiled=True)
    mid_parts = (
        [lower_mid[distance] for distance in range(mid_top, 0, -1)]
        + [pair_two]
        + [upper_mid[distance] for distance in range(1, mid_top + 1)]
    )
    mid_window = jnp.concatenate(mid_parts, axis=1)
    own_part = [pair_four] if near_far == 0 else []
    lower_window = jnp.concatenate(
        [lower_far[distance] for distance in range(far_top, far_low - 1, -1)] + own_part, axis=1
    )
    upper_window = jnp.concatenate(
        own_part + [upper_far[distance] for distance in range(far_low, far_top + 1)], axis=1
    )
    mid_side = (mid_top - 1) * blocks_dev + blocks_dev
    far_side = (far_top - 1) * blocks_dev + far_blocks
    coarse_block = POOL * jnp.arange(total_rows // POOL, dtype=jnp.int32) // BLOCK
    score_scale = 1.0 / math.sqrt(HEAD_DIM)
    mid_span = (MID_REACH - 1) * half_block
    far_span = (FAR_REACH - MID_REACH) * quarter_block

    def one_head(head_index, output):
        column = head_index * HEAD_DIM
        query_cols = lax.dynamic_slice_in_dim(queries, column, HEAD_DIM, 1).reshape(
            blocks_dev, BLOCK, HEAD_DIM
        )

        def head_cols(window_rows):
            sliced = lax.dynamic_slice_in_dim(window_rows, column, HEAD_DIM, 2)
            return (sliced[0], sliced[1])

        fine_pair = head_cols(fine_window)
        mid_pair = head_cols(mid_window)
        lower_pair = head_cols(lower_window)
        upper_pair = head_cols(upper_window)
        coarse_pair = head_cols(coarse_all)

        def block_attend(block_index, query_block):
            here = me_index * blocks_dev + block_index
            level_specs = [
                (fine_pair, block_index * BLOCK, 3 * BLOCK, here - 1, BLOCK, 0.0),
                (
                    mid_pair,
                    (mid_side + block_index - MID_REACH) * half_block,
                    mid_span,
                    here - MID_REACH,
                    half_block,
                    math.log(2.0),
                ),
                (
                    mid_pair,
                    (mid_side + block_index + 2) * half_block,
                    mid_span,
                    here + 2,
                    half_block,
                    math.log(2.0),
                ),
                (
                    lower_pair,
                    (far_side + block_index - FAR_REACH) * quarter_block,
                    far_span,
                    here - FAR_REACH,
                    quarter_block,
                    math.log(4.0),
                ),
                (
                    upper_pair,
                    (block_index + MID_REACH + 1 - near_far * blocks_dev) * quarter_block,
                    far_span,
                    here + MID_REACH + 1,
                    quarter_block,
                    math.log(4.0),
                ),
            ]
            level_items = []
            for pair_rows, anchor_row, span, first_block, unit_rows, log_size in level_specs:
                key_part = lax.dynamic_slice_in_dim(pair_rows[0], anchor_row, span, 0)
                value_part = lax.dynamic_slice_in_dim(pair_rows[1], anchor_row, span, 0)
                atom_block = first_block + jnp.arange(span, dtype=jnp.int32) // unit_rows
                allowed = (atom_block >= 0) & (atom_block < total_blocks)
                level_items.append((key_part, value_part, allowed, log_size))
            coarse_allowed = jnp.abs(coarse_block - here) > FAR_REACH
            level_items.append((coarse_pair[0], coarse_pair[1], coarse_allowed, math.log(POOL)))
            score_list = []
            for key_part, value_part, allowed, log_size in level_items:
                scores = (
                    jnp.einsum(
                        "qe,ke->qk", query_block, key_part, preferred_element_type=jnp.float32
                    )
                    * score_scale
                    + log_size
                )
                score_list.append(jnp.where(allowed[None, :], scores, -jnp.inf))
            row_top = reduce(jnp.maximum, [jnp.max(scores, axis=1) for scores in score_list])
            denominator = jnp.zeros((BLOCK,), jnp.float32)
            weighted = jnp.zeros((BLOCK, HEAD_DIM), jnp.float32)
            for scores, level_item in zip(score_list, level_items):
                exp_terms = jnp.exp(scores - row_top[:, None])
                denominator = denominator + jnp.sum(exp_terms, axis=1)
                weighted = weighted + jnp.dot(
                    exp_terms.astype(jnp.bfloat16),
                    level_item[1],
                    preferred_element_type=jnp.float32,
                )
            return (weighted / denominator[:, None]).astype(jnp.bfloat16)

        results = jax.vmap(block_attend)(jnp.arange(blocks_dev, dtype=jnp.int32), query_cols)
        return lax.dynamic_update_slice_in_dim(
            output, results.reshape(rows_dev, HEAD_DIM), column, 1
        )

    return lax.fori_loop(0, queries.shape[1] // HEAD_DIM, one_head, jnp.zeros_like(queries))


def solution(mesh):
    placed = (P("seq", "head"), P("seq", "head"), P("seq", "head"))
    return jax.shard_map(
        per_device, mesh=mesh, in_specs=placed, out_specs=P("seq", "head"), check_vma=False
    )
```

profile of v0, /device:TPU:0, one launch (start us, length us, event | category | flops | bytes accessed | tf_op | source)
XLA Modules:
  0.0 378.5 jit_solution(829424252145104084)
XLA Ops:
  0.0 1.8 stack.19
  3.6 1.4 fusion.87
  5.0 5.9 %collective-permute-start.2 = (bf16[2,128,2048]{2,1,0:T(8,128)(2,1)}, bf16[2,128,2048]{2,1,0:T(8,128)(2,1)}, u32[]{:S(2)}, u32[]{:S(2)}) collective-permute-start(bf16[2,128,2048]{2,1,0:T(8,128)(2,1)} %fusion.87), channel_id=1, source_target_pairs={{0,8},{4,12},{8,16},{12,20},{16,24},{20,28},{1,9},{5,13},{9,17},{1... | collective-permute-start | bytes 3145736 | tf_op jit(solution)/shard_map/ppermute | solution.py:19
  10.9 4.4 %collective-permute-start.3 = (bf16[2,128,2048]{2,1,0:T(8,128)(2,1)}, bf16[2,128,2048]{2,1,0:T(8,128)(2,1)}, u32[]{:S(2)}, u32[]{:S(2)}) collective-permute-start(bf16[2,128,2048]{2,1,0:T(8,128)(2,1)} %fusion.87), channel_id=1, source_target_pairs={{0,4},{4,8},{8,12},{12,16},{16,20},{20,24},{24,28},{1,5},{5,9},{9,... | collective-permute-start | bytes 3145736 | tf_op jit(solution)/shard_map/ppermute | solution.py:19
  15.3 1.3 collective-permute-start.4
  16.6 1.3 collective-permute-start.5
  17.9 1.5 fusion.53
  19.4 1.3 collective-permute-start.1
  20.7 1.5 fusion.52
  22.2 2.3 copy.47
  26.0 81.8 %all_gather.3 = bf16[2,32,2048]{2,0,1:T(2,128)(2,1)S(1)} all-gather(bf16[2,4,2048]{2,0,1:T(2,128)(2,1)S(1)} %multiply_convert_fusion), channel_id=1, replica_groups=mesh['seq'=8,'head'=4] {'seq'}, dimensions={1}, use_global_device_ids=true | all-gather | bytes 294912 | tf_op jit(solution)/shard_map/all_gather | solution.py:109
  108.8 3.1 collective-permute-start
  111.9 2.3 copy.49
  115.2 1.5 constant_dynamic-update-slice_fusion.5
  116.8 1.3 collective-permute-start.8
  118.1 1.3 constant_dynamic-update-slice_fusion.4
  119.9 5.0 %collective-permute-start.7 = (bf16[2,64,2048]{2,0,1:T(2,128)(2,1)S(1)}, bf16[2,64,2048]{2,0,1:T(2,128)(2,1)S(1)}, u32[]{:S(2)}, u32[]{:S(2)}) collective-permute-start(bf16[2,64,2048]{2,0,1:T(2,128)(2,1)S(1)} %fusion.86), channel_id=1, source_target_pairs={{0,16},{4,20},{8,24},{12,28},{1,17},{5,21},{9,25},{13,29},{2,18},{... | collective-permute-start | bytes 1572872 | tf_op jit(solution)/shard_map/ppermute | solution.py:19
  124.9 3.1 collective-permute-done
  128.0 13.3 %collective-permute-start.6 = (bf16[2,64,2048]{2,0,1:T(2,128)(2,1)S(1)}, bf16[2,64,2048]{2,0,1:T(2,128)(2,1)S(1)}, u32[]{:S(2)}, u32[]{:S(2)}) collective-permute-start(bf16[2,64,2048]{2,0,1:T(2,128)(2,1)S(1)} %fusion.86), channel_id=1, source_target_pairs={{0,20},{4,24},{8,28},{1,21},{5,25},{9,29},{2,22},{6,26},{10,30},{3... | collective-permute-start | bytes 1572872 | tf_op jit(solution)/shard_map/ppermute | solution.py:19
  141.3 3.3 pad_maximum_fusion
  144.6 1.3 collective-permute-start.11
  145.9 1.3 constant_dynamic-update-slice_fusion.2
  147.2 1.3 collective-permute-start.10
  148.5 1.5 collective-permute-start.9
  150.0 4.0 %pad_maximum_fusion.1 = bf16[2,256,2048]{2,0,1:T(2,128)(2,1)} fusion(bf16[2,64,2048]{2,0,1:T(2,128)(2,1)S(1)} %fusion.62, bf16[2,64,2048]{2,0,1:T(2,128)(2,1)S(1)} %collective-permute-done.8, bf16[2,64,2048]{2,0,1:T(2,128)(2,1)S(1)} %collective-permute-done.7, bf16[2,64,2048]{2,0,1:T(2,128)(2,1)S(1)} %collective-permute-done.6), kind=kLoop, calls=%fused_computation.138 | loop fusion | flops 3145728 | bytes 4194304 | tf_op jit(solution)/shard_map/concatenate | solution.py:117
  154.0 1.3 constant_dynamic-update-slice_fusion.1
  155.3 3.1 copy.52
  159.4 9.3 %collective-permute-done.11 = bf16[2,64,2048]{2,0,1:T(2,128)(2,1)S(1)} collective-permute-done((bf16[2,64,2048]{2,0,1:T(2,128)(2,1)S(1)}, bf16[2,64,2048]{2,0,1:T(2,128)(2,1)S(1)}, u32[]{:S(2)}, u32[]{:S(2)}) %collective-permute-start.11) | collective-permute-done | bytes 524320 | tf_op jit(solution)/shard_map/ppermute | solution.py:19
  168.7 32.8 %collective-permute-done.10 = bf16[2,64,2048]{2,0,1:T(2,128)(2,1)S(1)} collective-permute-done((bf16[2,64,2048]{2,0,1:T(2,128)(2,1)S(1)}, bf16[2,64,2048]{2,0,1:T(2,128)(2,1)S(1)}, u32[]{:S(2)}, u32[]{:S(2)}) %collective-permute-start.10) | collective-permute-done | bytes 524320 | tf_op jit(solution)/shard_map/ppermute | solution.py:19
  201.5 4.0 %pad_maximum_fusion.2 = bf16[2,256,2048]{2,0,1:T(2,128)(2,1)} fusion(bf16[2,64,2048]{2,0,1:T(2,128)(2,1)S(1)} %collective-permute-done.11, bf16[2,64,2048]{2,0,1:T(2,128)(2,1)S(1)} %collective-permute-done.10, bf16[2,64,2048]{2,0,1:T(2,128)(2,1)S(1)} %collective-permute-done.9, bf16[2,64,2048]{2,0,1:T(2,128)(2,1)S(1)} %fusion.63), kind=kLoop, calls=%fused_computation.139 | loop fusion | flops 3145728 | bytes 4194304 | tf_op jit(solution)/shard_map/concatenate | solution.py:120
  205.5 171.9 %while.59 = (s32[]{:T(128)}, bf16[256,2048]{1,0:T(8,128)(2,1)S(1)}, s32[]{:T(128)}, bf16[256,2048]{1,0:T(8,128)(2,1)}, bf16[2,512,2048]{2,1,0:T(8,128)(2,1)}, /*...) while((s32[]{:T(128)}, bf16[256,2048]{1,0:T(8,128)(2,1)S(1)}, ...), condition=%wide.region_14.15_spmd.clone, body=%wide.region_1.14_spmd.clone.sunk | while | flops 140719872 | bytes 10753917 | solution.py:220
  206.8 1.7 constant_dynamic-slice_fusion.32
  217.5 1.7 constant_dynamic-slice_fusion.32
  228.3 1.7 constant_dynamic-slice_fusion.32
  231.1 1.0 dynamic-slice_bitcast_fusion.6
  239.0 1.7 constant_dynamic-slice_fusion.32
  249.8 1.7 constant_dynamic-slice_fusion.32
  260.5 1.7 constant_dynamic-slice_fusion.32
  271.3 1.7 constant_dynamic-slice_fusion.32
  282.0 1.7 constant_dynamic-slice_fusion.32
  292.8 1.7 constant_dynamic-slice_fusion.32
  303.5 1.7 constant_dynamic-slice_fusion.32
  314.2 1.7 constant_dynamic-slice_fusion.32
  325.0 1.7 constant_dynamic-slice_fusion.32
  335.7 1.7 constant_dynamic-slice_fusion.32
  346.5 1.7 constant_dynamic-slice_fusion.32
  357.2 1.7 constant_dynamic-slice_fusion.32
  368.0 1.7 constant_dynamic-slice_fusion.32
  (1732 shorter events, 168.5 us)
Async XLA Ops:
  0.0 2.2 copy-start.2
  3.6 17.2 %copy-start = (f32[2,128,2,2048]{3,1,2,0:T(8,128)}, f32[2,128,2,2048]{3,1,2,0:T(8,128)S(1)}, u32[]{:S(2)}) copy-start(f32[2,128,2,2048]{3,1,2,0:T(8,128)S(1)} %maximum_convert_fusion) | copy-start | bytes 12582916
  3.6 14.3 %copy-start.3 = (bf16[256,2048]{1,0:T(8,128)(2,1)S(1)}, bf16[256,2048]{1,0:T(8,128)(2,1)}, u32[]{:S(2)}) copy-start(bf16[256,2048]{1,0:T(8,128)(2,1)} %param.7) | copy-start | bytes 3145732
  5.0 103.8 %collective-permute-start.2 = (bf16[2,128,2048]{2,1,0:T(8,128)(2,1)}, bf16[2,128,2048]{2,1,0:T(8,128)(2,1)}, u32[]{:S(2)}, u32[]{:S(2)}) collective-permute-start(bf16[2,128,2048]{2,1,0:T(8,128)(2,1)} %fusion.87), channel_id=1, source_target_pairs={{0,8},{4,12},{8,16},{12,20},{16,24},{20,28},{1,9},{5,13},{9,17},{1... | collective-permute-start | bytes 3145736 | tf_op jit(solution)/shard_map/ppermute | solution.py:19
  10.9 105.8 %collective-permute-start.3 = (bf16[2,128,2048]{2,1,0:T(8,128)(2,1)}, bf16[2,128,2048]{2,1,0:T(8,128)(2,1)}, u32[]{:S(2)}, u32[]{:S(2)}) collective-permute-start(bf16[2,128,2048]{2,1,0:T(8,128)(2,1)} %fusion.87), channel_id=1, source_target_pairs={{0,4},{4,8},{8,12},{12,16},{16,20},{20,24},{24,28},{1,5},{5,9},{9,... | collective-permute-start | bytes 3145736 | tf_op jit(solution)/shard_map/ppermute | solution.py:19
  15.3 129.2 %collective-permute-start.4 = (bf16[2,128,2048]{2,1,0:T(8,128)(2,1)}, bf16[2,128,2048]{2,1,0:T(8,128)(2,1)}, u32[]{:S(2)}, u32[]{:S(2)}) collective-permute-start(bf16[2,128,2048]{2,1,0:T(8,128)(2,1)} %fusion.87), channel_id=1, source_target_pairs={{4,0},{8,4},{12,8},{16,12},{20,16},{24,20},{28,24},{5,1},{9,5},{13... | collective-permute-start | bytes 3145736 | tf_op jit(solution)/shard_map/ppermute | solution.py:19
  16.6 137.4 %collective-permute-start.5 = (bf16[2,128,2048]{2,1,0:T(8,128)(2,1)}, bf16[2,128,2048]{2,1,0:T(8,128)(2,1)}, u32[]{:S(2)}, u32[]{:S(2)}) collective-permute-start(bf16[2,128,2048]{2,1,0:T(8,128)(2,1)} %fusion.87), channel_id=1, source_target_pairs={{8,0},{12,4},{16,8},{20,12},{24,16},{28,20},{9,1},{13,5},{17,9},{2... | collective-permute-start | bytes 3145736 | tf_op jit(solution)/shard_map/ppermute | solution.py:19
  19.4 100.4 %collective-permute-start.1 = (bf16[2,128,2048]{2,1,0:T(8,128)(2,1)}, bf16[2,128,2048]{2,1,0:T(8,128)(2,1)}, u32[]{:S(2)}, u32[]{:S(2)}) collective-permute-start(bf16[2,128,2048]{2,1,0:T(8,128)(2,1)} %get-tuple-element.677), channel_id=1, source_target_pairs={{4,0},{8,4},{12,8},{16,12},{20,16},{24,20},{28,24},{5,1},{9,5},{13... | collective-permute-start | bytes 3145736 | tf_op jit(solution)/shard_map/ppermute | solution.py:32
  26.0 82.8 %copy-start.7 = (bf16[2,128,2048]{2,1,0:T(8,128)(2,1)S(1)}, bf16[2,128,2048]{2,1,0:T(8,128)(2,1)}, u32[]{:S(2)}) copy-start(bf16[2,128,2048]{2,1,0:T(8,128)(2,1)} %get-tuple-element.676) | copy-start | bytes 3145732
  108.8 19.2 %collective-permute-start = (bf16[2,128,2048]{2,1,0:T(8,128)(2,1)S(1)}, bf16[2,128,2048]{2,1,0:T(8,128)(2,1)S(1)}, u32[]{:S(2)}, u32[]{:S(2)}) collective-permute-start(bf16[2,128,2048]{2,1,0:T(8,128)(2,1)S(1)} %copy-done.7), channel_id=1, source_target_pairs={{0,4},{4,8},{8,12},{12,16},{16,20},{20,24},{24,28},{1,5},{5,9},{9,... | collective-permute-start | bytes 3145736 | tf_op jit(solution)/shard_map/ppermute | solution.py:30
  114.2 5.2 %copy-start.1 = (f32[2,128,2,2048]{3,1,2,0:T(8,128)S(1)}, f32[2,128,2,2048]{3,1,2,0:T(8,128)}, u32[]{:S(2)}) copy-start(f32[2,128,2,2048]{3,1,2,0:T(8,128)} %copy-done) | copy-start | bytes 12582916
  116.8 30.4 %collective-permute-start.8 = (bf16[2,64,2048]{2,0,1:T(2,128)(2,1)S(1)}, bf16[2,64,2048]{2,0,1:T(2,128)(2,1)S(1)}, u32[]{:S(2)}, u32[]{:S(2)}) collective-permute-start(bf16[2,64,2048]{2,0,1:T(2,128)(2,1)S(1)} %fusion.86), channel_id=1, source_target_pairs={{0,12},{4,16},{8,20},{12,24},{16,28},{1,13},{5,17},{9,21},{13,25},... | collective-permute-start | bytes 1572872 | tf_op jit(solution)/shard_map/ppermute | solution.py:19
  119.4 21.8 %copy-start.4 = (bf16[256,2048]{1,0:T(8,128)(2,1)S(1)}, bf16[256,2048]{1,0:T(8,128)(2,1)}, u32[]{:S(2)}) copy-start(bf16[256,2048]{1,0:T(8,128)(2,1)} %param.7) | copy-start | bytes 3145732
  119.9 28.6 %collective-permute-start.7 = (bf16[2,64,2048]{2,0,1:T(2,128)(2,1)S(1)}, bf16[2,64,2048]{2,0,1:T(2,128)(2,1)S(1)}, u32[]{:S(2)}, u32[]{:S(2)}) collective-permute-start(bf16[2,64,2048]{2,0,1:T(2,128)(2,1)S(1)} %fusion.86), channel_id=1, source_target_pairs={{0,16},{4,20},{8,24},{12,28},{1,17},{5,21},{9,25},{13,29},{2,18},{... | collective-permute-start | bytes 1572872 | tf_op jit(solution)/shard_map/ppermute | solution.py:19
  128.0 22.0 %collective-permute-start.6 = (bf16[2,64,2048]{2,0,1:T(2,128)(2,1)S(1)}, bf16[2,64,2048]{2,0,1:T(2,128)(2,1)S(1)}, u32[]{:S(2)}, u32[]{:S(2)}) collective-permute-start(bf16[2,64,2048]{2,0,1:T(2,128)(2,1)S(1)} %fusion.86), channel_id=1, source_target_pairs={{0,20},{4,24},{8,28},{1,21},{5,25},{9,29},{2,22},{6,26},{10,30},{3... | collective-permute-start | bytes 1572872 | tf_op jit(solution)/shard_map/ppermute | solution.py:19
  144.6 24.1 %collective-permute-start.11 = (bf16[2,64,2048]{2,0,1:T(2,128)(2,1)S(1)}, bf16[2,64,2048]{2,0,1:T(2,128)(2,1)S(1)}, u32[]{:S(2)}, u32[]{:S(2)}) collective-permute-start(bf16[2,64,2048]{2,0,1:T(2,128)(2,1)S(1)} %fusion.86), channel_id=1, source_target_pairs={{20,0},{24,4},{28,8},{21,1},{25,5},{29,9},{22,2},{26,6},{30,10},{2... | collective-permute-start | bytes 1572872 | tf_op jit(solution)/shard_map/ppermute | solution.py:19
  147.2 54.3 %collective-permute-start.10 = (bf16[2,64,2048]{2,0,1:T(2,128)(2,1)S(1)}, bf16[2,64,2048]{2,0,1:T(2,128)(2,1)S(1)}, u32[]{:S(2)}, u32[]{:S(2)}) collective-permute-start(bf16[2,64,2048]{2,0,1:T(2,128)(2,1)S(1)} %fusion.86), channel_id=1, source_target_pairs={{16,0},{20,4},{24,8},{28,12},{17,1},{21,5},{25,9},{29,13},{18,2},{... | collective-permute-start | bytes 1572872 | tf_op jit(solution)/shard_map/ppermute | solution.py:19
  148.5 52.9 %collective-permute-start.9 = (bf16[2,64,2048]{2,0,1:T(2,128)(2,1)S(1)}, bf16[2,64,2048]{2,0,1:T(2,128)(2,1)S(1)}, u32[]{:S(2)}, u32[]{:S(2)}) collective-permute-start(bf16[2,64,2048]{2,0,1:T(2,128)(2,1)S(1)} %fusion.86), channel_id=1, source_target_pairs={{12,0},{16,4},{20,8},{24,12},{28,16},{13,1},{17,5},{21,9},{25,13},... | collective-permute-start | bytes 1572872 | tf_op jit(solution)/shard_map/ppermute | solution.py:19
  155.3 4.1 %copy-start.5 = (bf16[2,640,2048]{2,1,0:T(8,128)(2,1)}, bf16[2,640,2048]{2,1,0:T(8,128)(2,1)S(1)}, u32[]{:S(2)}) copy-start(bf16[2,640,2048]{2,1,0:T(8,128)(2,1)S(1)} %constant_dynamic-update-slice_fusion.1) | copy-start | bytes 15728644
  377.5 1.0 copy-start.6
where the time goes:
time: 385 us; the launch traced here: 378 us
  local copies, waits for them, and re-layouts  121 us (31%)
  blocking collectives  81.8 us (21%)
  waiting for transfers between devices  45.1 us (12%)
  matrix products  42.3 us (11%)
  starting transfers between devices  40.9 us (11%)
  other arithmetic  32.9 us (9%)
  loops' own time  13.8 us (4%)
    all_gather x1, blocking collectives, per_device(): coarse_all = lax.all_gather(pair_coarse, 'seq', axis=1, tiled=True)  81.8 us
    ppermute x10, waiting for transfers between devices, passed_along(): return lax.ppermute(block, axis, route)  42.1 us
    ppermute x10, starting transfers between devices, passed_along(): return lax.ppermute(block, axis, route)  36.6 us
    squeeze x32, local copies, waits for them, and re-layouts, head_cols(): return (sliced[0], sliced[1])  32.4 us
    slice x32, local copies, waits for them, and re-layouts, head_cols(): return (sliced[0], sliced[1])  29.4 us
    gather x640, local copies, waits for them, and re-layouts  23.6 us
    dot_general x96, matrix products, block_attend(): jnp.dot(exp_terms.astype(jnp.bfloat16), level_item[1], preferred_element_...  22 us
    dot_general x96, matrix products, block_attend(): jnp.einsum('qe,ke->qk', query_block, key_part, preferred_element_type=jnp...  20.4 us
  transfers between devices with their start and end apart: 12, of which 3 were waited for; matrix products, arithmetic and copies ran while one was open for 7% of the time, Pallas kernels for 0%

commit v1 on v0

v1 whole, which is shorter than its diff:
```python
import functools
import math

import jax
import jax.numpy as jnp
from jax import lax
from jax.experimental import pallas as pl
from jax.experimental.pallas import tpu as pltpu
from jax.sharding import PartitionSpec as P

HEAD_DIM = 128
BLOCK = 128
POOL = 64
MID_REACH = 3
FAR_REACH = 9

HALF = BLOCK // 2
QUARTER = BLOCK // 4
GROUP_BLOCKS = 4
GROUP_ROWS = GROUP_BLOCKS * BLOCK
COARSE_SLOT = 16
COARSE_USED = GROUP_ROWS // POOL

FINE_LOW, FINE_BLOCKS = -1, GROUP_BLOCKS + 2
MID_LOW, MID_BLOCKS = -MID_REACH, GROUP_BLOCKS + 2 * MID_REACH
FAR_LOW, FAR_BLOCKS = -FAR_REACH, GROUP_BLOCKS + 2 * FAR_REACH

KIND_K, KIND_V, KIND_Q, KIND_O = 0, 1, 2, 3
ROUTES = (
    (4, 1, "fine", 3, 1, -1),
    (5, -1, "fine", 0, 1, 4),
    (6, 1, "mid", 1, 2, -3),
    (7, -1, "mid", 1, 2, 5),
    (8, 2, "far", 0, 4, -8),
    (9, -2, "far", 0, 4, 8),
    (10, 1, "far", 0, 1, -4),
    (11, -1, "far", 3, 1, 7),
    (12, 3, "far", 3, 1, -9),
    (13, -3, "far", 0, 1, 12),
)
KINDS = 14
MESH = pl.DeviceIdType.MESH


def pool_matrix(out_rows, in_rows, group_rows, used_rows=None):
    row = lax.broadcasted_iota(jnp.int32, (out_rows, in_rows), 0)
    col = lax.broadcasted_iota(jnp.int32, (out_rows, in_rows), 1)
    return jnp.where(col // group_rows == row, 1.0 / group_rows, 0.0).astype(jnp.bfloat16)


def pooled(source, out_rows, group_rows):
    weights = pool_matrix(out_rows, source.shape[0], group_rows)
    return jnp.dot(weights, source, preferred_element_type=jnp.float32).astype(jnp.bfloat16)


def kernel(
    groups, q_ref, k_ref, v_ref, o_ref,
    q_rows, fine, mid, far, coarse, out_rows, out_back, bias,
    send, recv, coarse_send, coarse_recv,
):
    me = lax.axis_index("seq")
    group = me // 2
    parity = me % 2
    partner = me + 1 - 2 * parity
    rows_dev = q_ref.shape[0]
    chunks = q_rows.shape[0]
    half_cols = chunks * HEAD_DIM
    own_first = pl.multiple_of(parity * rows_dev, rows_dev)
    other_first = pl.multiple_of((1 - parity) * rows_dev, rows_dev)
    levels = {"fine": (fine, BLOCK, FINE_LOW), "mid": (mid, HALF, MID_LOW), "far": (far, QUARTER, FAR_LOW)}

    def own_cols(chunk):
        return pl.ds(pl.multiple_of(parity * half_cols + chunk * HEAD_DIM, HEAD_DIM), HEAD_DIM)

    def other_cols(chunk):
        return pl.ds(pl.multiple_of((1 - parity) * half_cols + chunk * HEAD_DIM, HEAD_DIM), HEAD_DIM)

    def remote(src, dst, kind, chunk, target):
        return pltpu.make_async_remote_copy(
            src_ref=src, dst_ref=dst, send_sem=send.at[chunk, kind], recv_sem=recv.at[chunk, kind],
            device_id={"seq": target}, device_id_type=MESH,
        )

    def exchange(kind, chunk):
        if kind == KIND_Q:
            return remote(
                q_ref.at[:, other_cols(chunk)], q_rows.at[chunk, pl.ds(own_first, rows_dev)],
                kind, chunk, partner,
            )
        if kind == KIND_O:
            return remote(
                out_rows.at[chunk, pl.ds(other_first, rows_dev)], out_back.at[chunk], kind, chunk, partner
            )
        source = k_ref if kind == KIND_K else v_ref
        return remote(
            source.at[:, other_cols(chunk)], fine.at[chunk, kind, pl.ds(BLOCK + own_first, rows_dev)],
            kind, chunk, partner,
        )

    def routed(route, chunk):
        kind, offset, level, first, count, landing = route
        window, unit, low = levels[level]
        return remote(
            window.at[chunk, :, pl.ds((first - low) * unit, count * unit)],
            window.at[chunk, :, pl.ds((landing - low) * unit, count * unit)],
            kind, chunk, me + 2 * offset,
        )

    def coarse_copy(chunk, step):
        target = lax.rem(group + step, groups) * 2 + parity
        slot = pl.ds(pl.multiple_of(group * COARSE_SLOT, COARSE_SLOT), COARSE_SLOT)
        return pltpu.make_async_remote_copy(
            src_ref=coarse.at[chunk, :, slot], dst_ref=coarse.at[chunk, :, slot],
            send_sem=coarse_send.at[chunk, step], recv_sem=coarse_recv.at[chunk, step],
            device_id={"seq": target}, device_id_type=MESH,
        )

    def inside(offset):
        return (group + offset >= 0) & (group + offset < groups)

    barrier = pltpu.get_barrier_semaphore()
    pl.semaphore_signal(barrier, inc=1, device_id={"seq": partner}, device_id_type=MESH)

    @pl.loop(1, groups)
    def _(step):
        target = lax.rem(group + step, groups) * 2 + parity
        pl.semaphore_signal(barrier, inc=1, device_id={"seq": target}, device_id_type=MESH)

    pl.semaphore_wait(barrier, groups)

    @pl.loop(0, chunks)
    def _(chunk):
        exchange(KIND_K, chunk).start()
        exchange(KIND_V, chunk).start()

    @pl.loop(0, chunks)
    def _(chunk):
        exchange(KIND_Q, chunk).start()

    for _, offset, level, _, count, landing in ROUTES:
        window, unit, low = levels[level]

        @pl.when(jnp.logical_not(inside(-offset)))
        def _():
            @pl.loop(0, chunks)
            def _(chunk):
                window[chunk, :, pl.ds((landing - low) * unit, count * unit)] = jnp.zeros(
                    (2, count * unit, HEAD_DIM), jnp.bfloat16
                )

    atoms = bias.shape[1]
    total_blocks = groups * GROUP_BLOCKS
    place = lax.broadcasted_iota(jnp.int32, (1, atoms), 1)
    windows_end = 8 * BLOCK
    for block in range(GROUP_BLOCKS):
        rel = jnp.where(
            place < 384,
            block - 1 + place // BLOCK,
            jnp.where(
                place < 512,
                block - 3 + (place - 384) // HALF,
                jnp.where(
                    place < 640,
                    block + 2 + (place - 512) // HALF,
                    jnp.where(
                        place < 832,
                        block - 9 + (place - 640) // QUARTER,
                        block + 4 + (place - 832) // QUARTER,
                    ),
                ),
            ),
        )
        here = group * GROUP_BLOCKS + rel
        held = (here >= 0) & (here < total_blocks)
        late = place - windows_end
        slot_row = late % COARSE_SLOT
        coarse_block = late // COARSE_SLOT * GROUP_BLOCKS + slot_row * POOL // BLOCK
        apart = jnp.abs(coarse_block - (group * GROUP_BLOCKS + block)) > FAR_REACH
        allowed = ((place < windows_end) & held) | (
            (place >= windows_end) & (slot_row < COARSE_USED) & apart
        )
        log_size = jnp.where(
            place < 384, 0.0, jnp.where(place < 640, 1.0, jnp.where(place < windows_end, 2.0, math.log2(POOL)))
        )
        bias[pl.ds(block, 1), :] = jnp.where(allowed, log_size, -jnp.inf)

    @pl.loop(0, chunks)
    def _(chunk):
        own = pl.ds(BLOCK + own_first, rows_dev)
        fine[chunk, 0, own] = k_ref[:, own_cols(chunk)]
        fine[chunk, 1, own] = v_ref[:, own_cols(chunk)]
        q_rows[chunk, pl.ds(own_first, rows_dev)] = q_ref[:, own_cols(chunk)]
        exchange(KIND_K, chunk).wait_recv()
        exchange(KIND_V, chunk).wait_recv()
        for route in ROUTES[:2]:
            @pl.when(inside(route[1]))
            def _():
                routed(route, chunk).start()
        slot = pl.ds(pl.multiple_of(group * COARSE_SLOT, COARSE_SLOT), COARSE_SLOT)
        for side in range(2):
            rows = fine[chunk, side, BLOCK : BLOCK + GROUP_ROWS]
            twos = pooled(rows, GROUP_ROWS // 2, 2)
            fours = pooled(twos, GROUP_ROWS // 4, 2)
            mid[chunk, side, -MID_LOW * HALF : (GROUP_BLOCKS - MID_LOW) * HALF] = twos
            far[chunk, side, -FAR_LOW * QUARTER : (GROUP_BLOCKS - FAR_LOW) * QUARTER] = fours
            coarse[chunk, side, slot] = pooled(fours, COARSE_SLOT, POOL // 4)
        for route in ROUTES[2:]:
            @pl.when(inside(route[1]))
            def _():
                routed(route, chunk).start()

        @pl.loop(1, groups)
        def _(step):
            coarse_copy(chunk, step).start()

    scale = math.log2(math.e) / math.sqrt(HEAD_DIM)

    @pl.loop(0, chunks)
    def _(chunk):
        exchange(KIND_Q, chunk).wait_recv()
        for route in ROUTES:
            @pl.when(inside(-route[1]))
            def _():
                routed(route, chunk).wait_recv()

        @pl.loop(1, groups)
        def _(step):
            origin = pl.ds(
                pl.multiple_of(lax.rem(group - step + groups, groups) * COARSE_SLOT, COARSE_SLOT), COARSE_SLOT
            )
            pltpu.make_async_remote_copy(
                src_ref=coarse.at[chunk, :, origin], dst_ref=coarse.at[chunk, :, origin],
                send_sem=coarse_send.at[chunk, step], recv_sem=coarse_recv.at[chunk, step],
                device_id={"seq": partner}, device_id_type=MESH,
            ).wait_recv()

        for side in range(2):
            mid[chunk, side, 2 * HALF : 3 * HALF] = pooled(fine[chunk, side, :BLOCK], HALF, 2)
            mid[chunk, side, 7 * HALF : 8 * HALF] = pooled(fine[chunk, side, 5 * BLOCK :], HALF, 2)
            far[chunk, side, 6 * QUARTER : 9 * QUARTER] = pooled(
                mid[chunk, side, : 3 * HALF], 3 * QUARTER, 2
            )
            far[chunk, side, 13 * QUARTER : 16 * QUARTER] = pooled(
                mid[chunk, side, 7 * HALF :], 3 * QUARTER, 2
            )

        for block in range(GROUP_BLOCKS):
            def atom_rows(side):
                return jnp.concatenate(
                    [
                        fine[chunk, side, block * BLOCK : (block + 3) * BLOCK],
                        mid[chunk, side, block * HALF : (block + 2) * HALF],
                        mid[chunk, side, (block + 5) * HALF : (block + 7) * HALF],
                        far[chunk, side, block * QUARTER : (block + 6) * QUARTER],
                        far[chunk, side, (block + 13) * QUARTER : (block + 19) * QUARTER],
                        coarse[chunk, side],
                    ],
                    axis=0,
                )

            scores = lax.dot_general(
                q_rows[chunk, block * BLOCK : (block + 1) * BLOCK], atom_rows(0),
                (((1,), (1,)), ((), ())), preferred_element_type=jnp.float32,
            ) * scale + bias[pl.ds(block, 1), :]
            row_top = jnp.max(scores, axis=1, keepdims=True)
            exp_terms = jnp.exp2(scores - row_top)
            denominator = jnp.sum(exp_terms, axis=1, keepdims=True)
            weighted = jnp.dot(
                exp_terms.astype(jnp.bfloat16), atom_rows(1), preferred_element_type=jnp.float32
            )
            out_rows[chunk, block * BLOCK : (block + 1) * BLOCK] = (weighted / denominator).astype(
                jnp.bfloat16
            )
        exchange(KIND_O, chunk).start()
        o_ref[:, own_cols(chunk)] = out_rows[chunk, pl.ds(own_first, rows_dev)]

    @pl.loop(0, chunks)
    def _(chunk):
        exchange(KIND_O, chunk).wait_recv()
        o_ref[:, other_cols(chunk)] = out_back[chunk]

    @pl.loop(0, chunks)
    def _(chunk):
        for kind in (KIND_K, KIND_V, KIND_Q, KIND_O):
            exchange(kind, chunk).wait_send()
        for route in ROUTES:
            @pl.when(inside(route[1]))
            def _():
                routed(route, chunk).wait_send()

        @pl.loop(1, groups)
        def _(step):
            coarse_copy(chunk, step).wait_send()


def per_device(queries, key_rows, value_rows):
    rows_dev, cols = queries.shape
    groups = lax.axis_size("seq") // 2
    chunks = cols // 2 // HEAD_DIM
    atoms = 8 * BLOCK + groups * COARSE_SLOT
    bf16 = jnp.bfloat16
    vmem = pl.BlockSpec(memory_space=pltpu.VMEM)
    return pl.pallas_call(
        functools.partial(kernel, groups),
        out_shape=jax.ShapeDtypeStruct(queries.shape, bf16),
        in_specs=[vmem] * 3,
        out_specs=vmem,
        scratch_shapes=[
            pltpu.VMEM((chunks, 2 * rows_dev, HEAD_DIM), bf16),
            pltpu.VMEM((chunks, 2, FINE_BLOCKS * BLOCK, HEAD_DIM), bf16),
            pltpu.VMEM((chunks, 2, MID_BLOCKS * HALF, HEAD_DIM), bf16),
            pltpu.VMEM((chunks, 2, FAR_BLOCKS * QUARTER, HEAD_DIM), bf16),
            pltpu.VMEM((chunks, 2, groups * COARSE_SLOT, HEAD_DIM), bf16),
            pltpu.VMEM((chunks, 2 * rows_dev, HEAD_DIM), bf16),
            pltpu.VMEM((chunks, rows_dev, HEAD_DIM), bf16),
            pltpu.VMEM((8, atoms), jnp.float32),
            pltpu.SemaphoreType.DMA((chunks, KINDS)),
            pltpu.SemaphoreType.DMA((chunks, KINDS)),
            pltpu.SemaphoreType.DMA((chunks, groups)),
            pltpu.SemaphoreType.DMA((chunks, groups)),
        ],
        compiler_params=pltpu.CompilerParams(
            collective_id=0, has_side_effects=True, vmem_limit_bytes=48 * 1024 * 1024
        ),
    )(queries, key_rows, value_rows)


def solution(mesh):
    placed = (P("seq", "head"), P("seq", "head"), P("seq", "head"))
    return jax.shard_map(
        per_device, mesh=mesh, in_specs=placed, out_specs=P("seq", "head"), check_vma=False
    )
```

time: 385 us -> 79.1 us (0.21); the launches traced: 378 us -> 78.9 us
  local copies, waits for them, and re-layouts: 121 us -> 4.65 us
  blocking collectives: 81.8 us -> 0 us
  Pallas kernels: 0 us -> 74.2 us
  waiting for transfers between devices: 45.1 us -> 0 us
  matrix products: 42.3 us -> 0 us
  starting transfers between devices: 40.9 us -> 0 us
  other arithmetic: 32.9 us -> 0 us
  loops' own time: 13.8 us -> 0 us
    all_gather x1 -> x0, blocking collectives: 81.8 us -> none  [per_device(): coarse_all = lax.all_gather(pair_coarse, 'seq', axis=1, tiled=True)]
    pallas_call x0 -> x1, Pallas kernels: none -> 74.2 us  [per_device(): pl.pallas_call(functools.partial(kernel, groups), out_shape=jax.ShapeDtyp...]
    ppermute x12 -> x0, waiting for transfers between devices: 45.1 us -> none  [the longest x10 42.1 us: passed_along(): return lax.ppermute(block, axis, route)]
    dot_general x192 -> x0, matrix products: 42.3 us -> none  [the longest x96 22 us: block_attend(): jnp.dot(exp_terms.astype(jnp.bfloat16), level_item[1], preferred_element_...]
    ppermute x12 -> x0, starting transfers between devices: 40.9 us -> none  [the longest x10 36.6 us: passed_along(): return lax.ppermute(block, axis, route)]
    squeeze x32 -> x0, local copies, waits for them, and re-layouts: 32.4 us -> none  [head_cols(): return (sliced[0], sliced[1])]
    slice x32 -> x0, local copies, waits for them, and re-layouts: 29.4 us -> none  [head_cols(): return (sliced[0], sliced[1])]
    gather x640 -> x0, local copies, waits for them, and re-layouts: 23.6 us -> none
  transfers between devices with their start and end apart: 12 -> 0, of which waited for: 3 -> 0; matrix products, arithmetic and copies ran while one was open for 7% -> 0% of each run, Pallas kernels for 0% -> 0%
where the time goes in v1:
time: 79.1 us; the launch traced here: 78.9 us
  Pallas kernels  74.2 us (94%)
  local copies, waits for them, and re-layouts  4.65 us (6%)
    pallas_call x1, Pallas kernels, per_device(): pl.pallas_call(functools.partial(kernel, groups), out_shape=jax.ShapeDtyp...  74.2 us
    unnamed x7, local copies, waits for them, and re-layouts  4.65 us

profile of v1, /device:TPU:0, one launch (start us, length us, event | category | flops | bytes accessed | tf_op | source)
XLA Modules:
  0.0 78.9 jit_solution(6201424005168437305)
XLA Ops:
  0.0 0.0 copy-start
  0.0 1.2 %copy-done = bf16[256,2048]{1,0:T(8,128)(2,1)S(1)} copy-done((bf16[256,2048]{1,0:T(8,128)(2,1)S(1)}, bf16[256,2048]{1,0:T(8,128)(2,1)}, u32[]{:S(2)}) %copy-start) | copy-done | bytes 1048600
  1.2 0.0 copy-start.1
  1.2 1.2 %copy-done.1 = bf16[256,2048]{1,0:T(8,128)(2,1)S(1)} copy-done((bf16[256,2048]{1,0:T(8,128)(2,1)S(1)}, bf16[256,2048]{1,0:T(8,128)(2,1)}, u32[]{:S(2)}) %copy-start.1) | copy-done | bytes 1048600
  2.5 0.0 copy-start.2
  2.5 1.2 %copy-done.2 = bf16[256,2048]{1,0:T(8,128)(2,1)S(1)} copy-done((bf16[256,2048]{1,0:T(8,128)(2,1)S(1)}, bf16[256,2048]{1,0:T(8,128)(2,1)}, u32[]{:S(2)}) %copy-start.2) | copy-done | bytes 1048600
  3.7 74.2 %shard_map.37 = bf16[256,2048]{1,0:T(8,128)(2,1)S(1)} custom-call(bf16[256,2048]{1,0:T(8,128)(2,1)S(1)} %copy-done, bf16[256,2048]{1,0:T(8,128)(2,1)S(1)} %copy-done.1, bf16[256,2048]{1,0:T(8,128)(2,1)S(1)} %copy-done.2), custom_call_target="tpu_custom_call" | custom-call | tf_op jit(solution)/shard_map/pallas_call | solution.py:303
  77.9 1.0 %copy.5 = bf16[256,2048]{1,0:T(8,128)(2,1)} copy(bf16[256,2048]{1,0:T(8,128)(2,1)S(1)} %shard_map.37) | data formatting | bytes 2097152
Async XLA Ops:
  0.0 1.2 %copy-start = (bf16[256,2048]{1,0:T(8,128)(2,1)S(1)}, bf16[256,2048]{1,0:T(8,128)(2,1)}, u32[]{:S(2)}) copy-start(bf16[256,2048]{1,0:T(8,128)(2,1)} %q_ref.1) | copy-start | bytes 3145732
  1.2 1.2 %copy-start.1 = (bf16[256,2048]{1,0:T(8,128)(2,1)S(1)}, bf16[256,2048]{1,0:T(8,128)(2,1)}, u32[]{:S(2)}) copy-start(bf16[256,2048]{1,0:T(8,128)(2,1)} %k_ref.1) | copy-start | bytes 3145732
  2.5 1.2 %copy-start.2 = (bf16[256,2048]{1,0:T(8,128)(2,1)S(1)}, bf16[256,2048]{1,0:T(8,128)(2,1)}, u32[]{:S(2)}) copy-start(bf16[256,2048]{1,0:T(8,128)(2,1)} %v_ref.1) | copy-start | bytes 3145732

commit v2 on v1

--- a/solution.py
+++ b/solution.py
@@ -26,23 +26,33 @@
 FAR_LOW, FAR_BLOCKS = -FAR_REACH, GROUP_BLOCKS + 2 * FAR_REACH
 
 KIND_K, KIND_V, KIND_Q, KIND_O = 0, 1, 2, 3
-ROUTES = (
+FIRST_HOP = (
     (4, 1, "fine", 3, 1, -1),
     (5, -1, "fine", 0, 1, 4),
     (6, 1, "mid", 1, 2, -3),
     (7, -1, "mid", 1, 2, 5),
-    (8, 2, "far", 0, 4, -8),
-    (9, -2, "far", 0, 4, 8),
-    (10, 1, "far", 0, 1, -4),
-    (11, -1, "far", 3, 1, 7),
-    (12, 3, "far", 3, 1, -9),
-    (13, -3, "far", 0, 1, 12),
+    (8, 1, "far", 0, 1, -4),
+    (9, -1, "far", 3, 1, 7),
 )
+SECOND_HOP = (
+    (10, 2, "far", -4, 4, -8),
+    (11, -2, "far", 4, 4, 8),
+)
+THIRD_HOP = (
+    (12, 3, "far", -5, 1, -9),
+    (13, -3, "far", 8, 1, 12),
+)
+ROUTES = FIRST_HOP + SECOND_HOP + THIRD_HOP
+RELAY_LAG, FORWARD_LAG, ATTEND_LAG = 2, 3, 4
 KINDS = 14
 MESH = pl.DeviceIdType.MESH
 
 
-def pool_matrix(out_rows, in_rows, group_rows, used_rows=None):
+def hop_of(offset):
+    return 1 if offset > 0 else -1
+
+
+def pool_matrix(out_rows, in_rows, group_rows):
     row = lax.broadcasted_iota(jnp.int32, (out_rows, in_rows), 0)
     col = lax.broadcasted_iota(jnp.int32, (out_rows, in_rows), 1)
     return jnp.where(col // group_rows == row, 1.0 / group_rows, 0.0).astype(jnp.bfloat16)
@@ -55,8 +65,8 @@
 
 def kernel(
     groups, q_ref, k_ref, v_ref, o_ref,
-    q_rows, fine, mid, far, coarse, out_rows, out_back, bias,
-    send, recv, coarse_send, coarse_recv,
+    q_rows, fine, mid, far, coarse, out_rows, bias,
+    send, recv, coarse_send, coarse_recv, local,
 ):
     me = lax.axis_index("seq")
     group = me // 2
@@ -89,7 +99,8 @@
             )
         if kind == KIND_O:
             return remote(
-                out_rows.at[chunk, pl.ds(other_first, rows_dev)], out_back.at[chunk], kind, chunk, partner
+                out_rows.at[chunk, pl.ds(other_first, rows_dev)], o_ref.at[:, own_cols(chunk)],
+                kind, chunk, partner,
             )
         source = k_ref if kind == KIND_K else v_ref
         return remote(
@@ -103,7 +114,7 @@
         return remote(
             window.at[chunk, :, pl.ds((first - low) * unit, count * unit)],
             window.at[chunk, :, pl.ds((landing - low) * unit, count * unit)],
-            kind, chunk, me + 2 * offset,
+            kind, chunk, me + 2 * hop_of(offset),
         )
 
     def coarse_copy(chunk, step):
@@ -118,6 +129,34 @@
     def inside(offset):
         return (group + offset >= 0) & (group + offset < groups)
 
+    def start_routes(routes, chunk):
+        for route in routes:
+            hop = hop_of(route[1])
+
+            @pl.when(inside(hop) & inside(hop - route[1]))
+            def _():
+                routed(route, chunk).start()
+
+    def await_routes(routes, chunk):
+        for route in routes:
+            @pl.when(inside(-route[1]))
+            def _():
+                routed(route, chunk).wait_recv()
+
+    def own_copy(kind, chunk):
+        if kind == KIND_Q:
+            source, target = q_ref, q_rows.at[chunk, pl.ds(own_first, rows_dev)]
+        else:
+            source = k_ref if kind == KIND_K else v_ref
+            target = fine.at[chunk, kind, pl.ds(BLOCK + own_first, rows_dev)]
+        return pltpu.make_async_copy(source.at[:, own_cols(chunk)], target, local.at[chunk, kind])
+
+    def own_result(chunk):
+        return pltpu.make_async_copy(
+            out_rows.at[chunk, pl.ds(own_first, rows_dev)], o_ref.at[:, own_cols(chunk)],
+            local.at[chunk, KIND_O],
+        )
+
     barrier = pltpu.get_barrier_semaphore()
     pl.semaphore_signal(barrier, inc=1, device_id={"seq": partner}, device_id_type=MESH)
 
@@ -132,10 +171,13 @@
     def _(chunk):
         exchange(KIND_K, chunk).start()
         exchange(KIND_V, chunk).start()
+        own_copy(KIND_K, chunk).start()
+        own_copy(KIND_V, chunk).start()
 
     @pl.loop(0, chunks)
     def _(chunk):
         exchange(KIND_Q, chunk).start()
+        own_copy(KIND_Q, chunk).start()
 
     for _, offset, level, _, count, landing in ROUTES:
         window, unit, low = levels[level]
@@ -184,18 +226,11 @@
         )
         bias[pl.ds(block, 1), :] = jnp.where(allowed, log_size, -jnp.inf)
 
-    @pl.loop(0, chunks)
-    def _(chunk):
-        own = pl.ds(BLOCK + own_first, rows_dev)
-        fine[chunk, 0, own] = k_ref[:, own_cols(chunk)]
-        fine[chunk, 1, own] = v_ref[:, own_cols(chunk)]
-        q_rows[chunk, pl.ds(own_first, rows_dev)] = q_ref[:, own_cols(chunk)]
-        exchange(KIND_K, chunk).wait_recv()
-        exchange(KIND_V, chunk).wait_recv()
-        for route in ROUTES[:2]:
-            @pl.when(inside(route[1]))
-            def _():
-                routed(route, chunk).start()
+    def gather(chunk):
+        for kind in (KIND_K, KIND_V):
+            own_copy(kind, chunk).wait()
+            exchange(kind, chunk).wait_recv()
+        start_routes(FIRST_HOP[:2], chunk)
         slot = pl.ds(pl.multiple_of(group * COARSE_SLOT, COARSE_SLOT), COARSE_SLOT)
         for side in range(2):
             rows = fine[chunk, side, BLOCK : BLOCK + GROUP_ROWS]
@@ -204,24 +239,35 @@
             mid[chunk, side, -MID_LOW * HALF : (GROUP_BLOCKS - MID_LOW) * HALF] = twos
             far[chunk, side, -FAR_LOW * QUARTER : (GROUP_BLOCKS - FAR_LOW) * QUARTER] = fours
             coarse[chunk, side, slot] = pooled(fours, COARSE_SLOT, POOL // 4)
-        for route in ROUTES[2:]:
-            @pl.when(inside(route[1]))
-            def _():
-                routed(route, chunk).start()
+        start_routes(FIRST_HOP[2:], chunk)
 
         @pl.loop(1, groups)
         def _(step):
             coarse_copy(chunk, step).start()
 
+    def relay(chunk):
+        await_routes(FIRST_HOP, chunk)
+        for side in range(2):
+            mid[chunk, side, 2 * HALF : 3 * HALF] = pooled(fine[chunk, side, :BLOCK], HALF, 2)
+            mid[chunk, side, 7 * HALF : 8 * HALF] = pooled(fine[chunk, side, 5 * BLOCK :], HALF, 2)
+            far[chunk, side, 6 * QUARTER : 9 * QUARTER] = pooled(
+                mid[chunk, side, : 3 * HALF], 3 * QUARTER, 2
+            )
+            far[chunk, side, 13 * QUARTER : 16 * QUARTER] = pooled(
+                mid[chunk, side, 7 * HALF :], 3 * QUARTER, 2
+            )
+        start_routes(SECOND_HOP, chunk)
+
+    def forward(chunk):
+        await_routes(SECOND_HOP, chunk)
+        start_routes(THIRD_HOP, chunk)
+
     scale = math.log2(math.e) / math.sqrt(HEAD_DIM)
 
-    @pl.loop(0, chunks)
-    def _(chunk):
+    def attend(chunk):
+        own_copy(KIND_Q, chunk).wait()
         exchange(KIND_Q, chunk).wait_recv()
-        for route in ROUTES:
-            @pl.when(inside(-route[1]))
-            def _():
-                routed(route, chunk).wait_recv()
+        await_routes(THIRD_HOP, chunk)
 
         @pl.loop(1, groups)
         def _(step):
@@ -233,16 +279,6 @@
                 send_sem=coarse_send.at[chunk, step], recv_sem=coarse_recv.at[chunk, step],
                 device_id={"seq": partner}, device_id_type=MESH,
             ).wait_recv()
-
-        for side in range(2):
-            mid[chunk, side, 2 * HALF : 3 * HALF] = pooled(fine[chunk, side, :BLOCK], HALF, 2)
-            mid[chunk, side, 7 * HALF : 8 * HALF] = pooled(fine[chunk, side, 5 * BLOCK :], HALF, 2)
-            far[chunk, side, 6 * QUARTER : 9 * QUARTER] = pooled(
-                mid[chunk, side, : 3 * HALF], 3 * QUARTER, 2
-            )
-            far[chunk, side, 13 * QUARTER : 16 * QUARTER] = pooled(
-                mid[chunk, side, 7 * HALF :], 3 * QUARTER, 2
-            )
 
         for block in range(GROUP_BLOCKS):
             def atom_rows(side):
@@ -272,19 +308,27 @@
                 jnp.bfloat16
             )
         exchange(KIND_O, chunk).start()
-        o_ref[:, own_cols(chunk)] = out_rows[chunk, pl.ds(own_first, rows_dev)]
+        own_result(chunk).start()
+
+    stages = ((gather, 0), (relay, RELAY_LAG), (forward, FORWARD_LAG), (attend, ATTEND_LAG))
+
+    @pl.loop(0, chunks + ATTEND_LAG)
+    def _(step):
+        for stage, lag in stages:
+            @pl.when((step >= lag) & (step < chunks + lag))
+            def _():
+                stage(step - lag)
 
     @pl.loop(0, chunks)
     def _(chunk):
+        own_result(chunk).wait()
         exchange(KIND_O, chunk).wait_recv()
-        o_ref[:, other_cols(chunk)] = out_back[chunk]
-
-    @pl.loop(0, chunks)
-    def _(chunk):
         for kind in (KIND_K, KIND_V, KIND_Q, KIND_O):
             exchange(kind, chunk).wait_send()
         for route in ROUTES:
-            @pl.when(inside(route[1]))
+            hop = hop_of(route[1])
+
+            @pl.when(inside(hop) & inside(hop - route[1]))
             def _():
                 routed(route, chunk).wait_send()
 
@@ -299,12 +343,12 @@
     chunks = cols // 2 // HEAD_DIM
     atoms = 8 * BLOCK + groups * COARSE_SLOT
     bf16 = jnp.bfloat16
-    vmem = pl.BlockSpec(memory_space=pltpu.VMEM)
+    placed = pl.BlockSpec(memory_space=pltpu.HBM)
     return pl.pallas_call(
         functools.partial(kernel, groups),
         out_shape=jax.ShapeDtypeStruct(queries.shape, bf16),
-        in_specs=[vmem] * 3,
-        out_specs=vmem,
+        in_specs=[placed] * 3,
+        out_specs=placed,
         scratch_shapes=[
             pltpu.VMEM((chunks, 2 * rows_dev, HEAD_DIM), bf16),
             pltpu.VMEM((chunks, 2, FINE_BLOCKS * BLOCK, HEAD_DIM), bf16),
@@ -312,12 +356,12 @@
             pltpu.VMEM((chunks, 2, FAR_BLOCKS * QUARTER, HEAD_DIM), bf16),
             pltpu.VMEM((chunks, 2, groups * COARSE_SLOT, HEAD_DIM), bf16),
             pltpu.VMEM((chunks, 2 * rows_dev, HEAD_DIM), bf16),
-            pltpu.VMEM((chunks, rows_dev, HEAD_DIM), bf16),
             pltpu.VMEM((8, atoms), jnp.float32),
             pltpu.SemaphoreType.DMA((chunks, KINDS)),
             pltpu.SemaphoreType.DMA((chunks, KINDS)),
             pltpu.SemaphoreType.DMA((chunks, groups)),
             pltpu.SemaphoreType.DMA((chunks, groups)),
+            pltpu.SemaphoreType.DMA((chunks, 4)),
         ],
         compiler_params=pltpu.CompilerParams(
             collective_id=0, has_side_effects=True, vmem_limit_bytes=48 * 1024 * 1024

time: 79.1 us -> 71.6 us (0.905)
  Pallas kernels: 74.2 us -> 66.8 us
    pallas_call x1, Pallas kernels: 74.2 us -> 66.8 us  [per_device(): pl.pallas_call(functools.partial(kernel, groups), out_shape=jax.ShapeDtyp...]
where the time goes in v2:
time: 71.6 us; the launch traced here: 71.4 us
  Pallas kernels  66.8 us (93%)
  local copies, waits for them, and re-layouts  4.65 us (6%)
    pallas_call x1, Pallas kernels, per_device(): pl.pallas_call(functools.partial(kernel, groups), out_shape=jax.ShapeDtyp...  66.8 us
    unnamed x7, local copies, waits for them, and re-layouts  4.65 us

profile of v2, /device:TPU:0, one launch (start us, length us, event | category | flops | bytes accessed | tf_op | source)
XLA Modules:
  0.0 71.4 jit_solution(4171885767175825961)
XLA Ops:
  0.0 0.0 copy-start
  0.0 1.2 %copy-done = bf16[256,2048]{1,0:T(8,128)(2,1)S(1)} copy-done((bf16[256,2048]{1,0:T(8,128)(2,1)S(1)}, bf16[256,2048]{1,0:T(8,128)(2,1)}, u32[]{:S(2)}) %copy-start) | copy-done | bytes 1048600
  1.2 0.0 copy-start.1
  1.2 1.2 %copy-done.1 = bf16[256,2048]{1,0:T(8,128)(2,1)S(1)} copy-done((bf16[256,2048]{1,0:T(8,128)(2,1)S(1)}, bf16[256,2048]{1,0:T(8,128)(2,1)}, u32[]{:S(2)}) %copy-start.1) | copy-done | bytes 1048600
  2.5 0.0 copy-start.2
  2.5 1.2 %copy-done.2 = bf16[256,2048]{1,0:T(8,128)(2,1)S(1)} copy-done((bf16[256,2048]{1,0:T(8,128)(2,1)S(1)}, bf16[256,2048]{1,0:T(8,128)(2,1)}, u32[]{:S(2)}) %copy-start.2) | copy-done | bytes 1048600
  3.7 66.8 %shard_map.37 = bf16[256,2048]{1,0:T(8,128)(2,1)S(1)} custom-call(bf16[256,2048]{1,0:T(8,128)(2,1)S(1)} %copy-done, bf16[256,2048]{1,0:T(8,128)(2,1)S(1)} %copy-done.1, bf16[256,2048]{1,0:T(8,128)(2,1)S(1)} %copy-done.2), custom_call_target="tpu_custom_call" | custom-call | tf_op jit(solution)/shard_map/pallas_call | solution.py:347
  70.4 1.0 %copy.5 = bf16[256,2048]{1,0:T(8,128)(2,1)} copy(bf16[256,2048]{1,0:T(8,128)(2,1)S(1)} %shard_map.37) | data formatting | bytes 2097152
Async XLA Ops:
  0.0 1.2 %copy-start = (bf16[256,2048]{1,0:T(8,128)(2,1)S(1)}, bf16[256,2048]{1,0:T(8,128)(2,1)}, u32[]{:S(2)}) copy-start(bf16[256,2048]{1,0:T(8,128)(2,1)} %q_ref.1) | copy-start | bytes 3145732
  1.2 1.2 %copy-start.1 = (bf16[256,2048]{1,0:T(8,128)(2,1)S(1)}, bf16[256,2048]{1,0:T(8,128)(2,1)}, u32[]{:S(2)}) copy-start(bf16[256,2048]{1,0:T(8,128)(2,1)} %k_ref.1) | copy-start | bytes 3145732
  2.5 1.2 %copy-start.2 = (bf16[256,2048]{1,0:T(8,128)(2,1)S(1)}, bf16[256,2048]{1,0:T(8,128)(2,1)}, u32[]{:S(2)}) copy-start(bf16[256,2048]{1,0:T(8,128)(2,1)} %v_ref.1) | copy-start | bytes 3145732

commit v3 on v2

--- a/solution.py
+++ b/solution.py
@@ -243,7 +243,9 @@
 
         @pl.loop(1, groups)
         def _(step):
-            coarse_copy(chunk, step).start()
+            @pl.when(jnp.abs(lax.rem(group + step, groups) - group) > 2)
+            def _():
+                coarse_copy(chunk, step).start()
 
     def relay(chunk):
         await_routes(FIRST_HOP, chunk)
@@ -271,14 +273,25 @@
 
         @pl.loop(1, groups)
         def _(step):
-            origin = pl.ds(
-                pl.multiple_of(lax.rem(group - step + groups, groups) * COARSE_SLOT, COARSE_SLOT), COARSE_SLOT
-            )
-            pltpu.make_async_remote_copy(
-                src_ref=coarse.at[chunk, :, origin], dst_ref=coarse.at[chunk, :, origin],
-                send_sem=coarse_send.at[chunk, step], recv_sem=coarse_recv.at[chunk, step],
-                device_id={"seq": partner}, device_id_type=MESH,
-            ).wait_recv()
+            giver = lax.rem(group - step + groups, groups)
+            origin = pl.ds(pl.multiple_of(giver * COARSE_SLOT, COARSE_SLOT), COARSE_SLOT)
+
+            @pl.when(jnp.abs(giver - group) > 2)
+            def _():
+                pltpu.make_async_remote_copy(
+                    src_ref=coarse.at[chunk, :, origin], dst_ref=coarse.at[chunk, :, origin],
+                    send_sem=coarse_send.at[chunk, step], recv_sem=coarse_recv.at[chunk, step],
+                    device_id={"seq": partner}, device_id_type=MESH,
+                ).wait_recv()
+
+        for offset in (-2, -1, 1, 2):
+            @pl.when(inside(offset))
+            def _():
+                near = pl.ds(pl.multiple_of((group + offset) * COARSE_SLOT, COARSE_SLOT), COARSE_SLOT)
+                first = (offset * GROUP_BLOCKS - FAR_LOW) * QUARTER
+                for side in range(2):
+                    fours = far[chunk, side, first : first + GROUP_ROWS // 4]
+                    coarse[chunk, side, near] = pooled(fours, COARSE_SLOT, POOL // 4)
 
         for block in range(GROUP_BLOCKS):
             def atom_rows(side):
@@ -334,7 +347,9 @@
 
         @pl.loop(1, groups)
         def _(step):
-            coarse_copy(chunk, step).wait_send()
+            @pl.when(jnp.abs(lax.rem(group + step, groups) - group) > 2)
+            def _():
+                coarse_copy(chunk, step).wait_send()
 
 
 def per_device(queries, key_rows, value_rows):

time: 71.6 us -> 70 us (0.978)
  Pallas kernels: 66.8 us -> 65.1 us
    pallas_call x1, Pallas kernels: 66.8 us -> 65.1 us  [per_device(): pl.pallas_call(functools.partial(kernel, groups), out_shape=jax.ShapeDtyp...]
where the time goes in v3:
time: 70 us; the launch traced here: 69.8 us
  Pallas kernels  65.1 us (93%)
  local copies, waits for them, and re-layouts  4.65 us (7%)
    pallas_call x1, Pallas kernels, per_device(): pl.pallas_call(functools.partial(kernel, groups), out_shape=jax.ShapeDtyp...  65.1 us
    unnamed x7, local copies, waits for them, and re-layouts  4.65 us

profile of v3, /device:TPU:0, one launch (start us, length us, event | category | flops | bytes accessed | tf_op | source)
XLA Modules:
  0.0 69.8 jit_solution(3827396898510887303)
XLA Ops:
  0.0 0.0 copy-start
  0.0 1.2 %copy-done = bf16[256,2048]{1,0:T(8,128)(2,1)S(1)} copy-done((bf16[256,2048]{1,0:T(8,128)(2,1)S(1)}, bf16[256,2048]{1,0:T(8,128)(2,1)}, u32[]{:S(2)}) %copy-start) | copy-done | bytes 1048600
  1.2 0.0 copy-start.1
  1.2 1.2 %copy-done.1 = bf16[256,2048]{1,0:T(8,128)(2,1)S(1)} copy-done((bf16[256,2048]{1,0:T(8,128)(2,1)S(1)}, bf16[256,2048]{1,0:T(8,128)(2,1)}, u32[]{:S(2)}) %copy-start.1) | copy-done | bytes 1048600
  2.5 0.0 copy-start.2
  2.5 1.2 %copy-done.2 = bf16[256,2048]{1,0:T(8,128)(2,1)S(1)} copy-done((bf16[256,2048]{1,0:T(8,128)(2,1)S(1)}, bf16[256,2048]{1,0:T(8,128)(2,1)}, u32[]{:S(2)}) %copy-start.2) | copy-done | bytes 1048600
  3.7 65.1 %shard_map.37 = bf16[256,2048]{1,0:T(8,128)(2,1)S(1)} custom-call(bf16[256,2048]{1,0:T(8,128)(2,1)S(1)} %copy-done, bf16[256,2048]{1,0:T(8,128)(2,1)S(1)} %copy-done.1, bf16[256,2048]{1,0:T(8,128)(2,1)S(1)} %copy-done.2), custom_call_target="tpu_custom_call" | custom-call | tf_op jit(solution)/shard_map/pallas_call | solution.py:362
  68.8 1.0 %copy.5 = bf16[256,2048]{1,0:T(8,128)(2,1)} copy(bf16[256,2048]{1,0:T(8,128)(2,1)S(1)} %shard_map.37) | data formatting | bytes 2097152
Async XLA Ops:
  0.0 1.2 %copy-start = (bf16[256,2048]{1,0:T(8,128)(2,1)S(1)}, bf16[256,2048]{1,0:T(8,128)(2,1)}, u32[]{:S(2)}) copy-start(bf16[256,2048]{1,0:T(8,128)(2,1)} %q_ref.1) | copy-start | bytes 3145732
  1.2 1.2 %copy-start.1 = (bf16[256,2048]{1,0:T(8,128)(2,1)S(1)}, bf16[256,2048]{1,0:T(8,128)(2,1)}, u32[]{:S(2)}) copy-start(bf16[256,2048]{1,0:T(8,128)(2,1)} %k_ref.1) | copy-start | bytes 3145732
  2.5 1.2 %copy-start.2 = (bf16[256,2048]{1,0:T(8,128)(2,1)S(1)}, bf16[256,2048]{1,0:T(8,128)(2,1)}, u32[]{:S(2)}) copy-start(bf16[256,2048]{1,0:T(8,128)(2,1)} %v_ref.1) | copy-start | bytes 3145732
